TPU v7x, 128 devices: a whole 4x4x4 slice. The times are simulated.
128 devices in a mesh: gx: 4 (over z), gy: 4 (over y), gz: 8 (over x, core).
Axes of the slice: x: 4, y: 4, z: 4, core: 2. Of those that a mesh axis runs over, the one named last changes fastest.
Arguments:
- positions: float32 [3, 64, 64, 2048], P(None, 'gx', 'gy', 'gz'), may hold values from -6 to 6
- pair_node: int32 [4, 4, 8, 32, 256], P('gx', 'gy', 'gz'), may hold values from 0 to 255
- pair_line: int32 [4, 4, 8, 32], P('gx', 'gy', 'gz'), may hold values from 0 to 255
- pair_far: int32 [4, 4, 8, 32, 256], P('gx', 'gy', 'gz'), may hold values from 0 to 261, as said below
- far_line: int32 [4, 4, 8, 32], P('gx', 'gy', 'gz'), may hold values from 0 to 483, as said below
- pair_geom: float32 [4, 4, 8, 32, 4, 256], P('gx', 'gy', 'gz'), may hold values from -4 to 4
- live_blocks: int32 [4, 4, 8], P('gx', 'gy', 'gz'), may hold values from 8 to 32, as said below
Outputs:
- corrected: float32 [3, 64, 64, 2048], P(None, 'gx', 'gy', 'gz')
- sweep_history: float32 [2, 5], replicated
Inputs may be any that keep to these rules, and one draw needn't show every extreme that they name: `pair_far`: together with far_line: at most one of the three coordinates of node b lies outside the owner block's own nodes; node b lies inside the whole grid; in slots below 16 node b is one of the owner block's own nodes. `far_line`: together with pair_far, as stated there. `live_blocks`: some owner block has all 32 slots live.
All inputs are finite; a program needn't handle non-finite values.
Results may differ from a plain program's by a relative error of at most 0.0001.
Values sent between devices are 32-bit elements; how exact they have to be, the bound alone decides.
No kernel may reach another device: no remote copies, remote signals or barrier semaphores. Data moves between devices by JAX's collectives and lax.ppermute only.
A program may use at most 64 MiB of HBM per device.

v0:
```python
import math
import jax
import jax.numpy as jnp
from jax import lax
from jax.sharding import Mesh
from jax.sharding import PartitionSpec as P

RIM = 3
SWEEPS = 5
GZ = ("gz_0", "gz_1")
GX_GY_GZ = ("gx", "gy", "gz_0", "gz_1")
relax_factor = 0.9
highest = lax.Precision.HIGHEST


def extended(cells, sides, width):
    for axis, dim in sides:
        count = lax.axis_size(axis)
        ends = count - 1
        head = lax.slice_in_dim(cells, 0, width, axis=dim)
        tail = lax.slice_in_dim(cells, cells.shape[dim] - width, cells.shape[dim], axis=dim)
        cells = jnp.concatenate(
            [
                lax.ppermute(tail, axis, [(i, (i + 1) % count) for i in range(ends)]),
                cells,
                lax.ppermute(head, axis, [((i + 1) % count, i) for i in range(ends)]),
            ],
            axis=dim,
        )
    return cells


def one_axis_at_a_time(x, axes):
    for axis in axes:
        x = lax.psum(x, axis)
    return x


def with_halo(x, sides, width):
    edges = {}
    for axis, dim in sides:
        count, length = (lax.axis_size(axis), x.shape[dim])
        up = [(i, (i + 1) % count) for i in range(count - 1)]
        last = lax.slice_in_dim(x, length - width, length, axis=dim)
        first = lax.slice_in_dim(x, 0, width, axis=dim)
        edges[dim] = (
            lax.ppermute(last, axis, up),
            lax.ppermute(first, axis, [(b, a) for a, b in up]),
        )
    done = []
    for _, dim in sides:
        low, high = edges[dim]
        around = [(width, width) if d in done else (0, 0) for d in range(x.ndim)]
        x = jnp.concatenate([jnp.pad(low, around), x, jnp.pad(high, around)], axis=dim)
        done.append(dim)
    return x


def node_sums(contribs, within, line_index, line_length, count_lines):
    blocks = contribs.shape[0]
    group_size = math.gcd(16, blocks)
    row_count = contribs.shape[1]
    columns = lax.broadcasted_iota(jnp.int32, (1, 1, line_length), 2)
    line_ids = lax.broadcasted_iota(jnp.int32, (1, count_lines), 1)

    def node_add_group(turn_idx, running):
        first_block = turn_idx * group_size
        term_part = lax.dynamic_slice_in_dim(contribs, first_block, group_size, 0)
        node_part = lax.dynamic_slice_in_dim(within, first_block, group_size, 0)
        line_part = lax.dynamic_slice_in_dim(line_index, first_block, group_size, 0)
        one_hot = (node_part[:, :, None] == columns).astype(jnp.float32)
        window = jnp.einsum("bcp,bpn->bcn", term_part, one_hot, precision=highest)
        line_hot = (line_part[:, None] == line_ids).astype(jnp.float32)
        return running + jnp.einsum("bl,bcn->cln", line_hot, window, precision=highest)

    initial = jnp.zeros((row_count, count_lines, line_length), jnp.float32)
    return lax.fori_loop(0, blocks // group_size, node_add_group, initial)


def select_lines(line_hot, field_lines):
    return jnp.einsum("bl,cln->bcn", line_hot, field_lines, precision=highest)


def sweep_terms(
    near_lines, far_lines, within, far_pos, line_index, geometry, live_mask, count_lines
):
    blocks = within.shape[0]
    group_size = math.gcd(16, blocks)
    near_cols = lax.broadcasted_iota(jnp.int32, (1, 1, near_lines.shape[2]), 2)
    far_cols = lax.broadcasted_iota(jnp.int32, (1, 1, far_lines.shape[2]), 2)
    line_ids = lax.broadcasted_iota(jnp.int32, (1, count_lines), 1)

    def sweep_add_group(turn_idx, carry):
        running, energy_sum = carry
        near_hot = (within[:, :, None] == near_cols).astype(jnp.float32)
        far_hot = (far_pos[:, :, None] == far_cols).astype(jnp.float32)
        near_vals = jnp.einsum("bcn,bpn->bcp", near_lines, near_hot, precision=highest)
        far_vals = jnp.einsum("bcn,bpn->bcp", far_lines, far_hot, precision=highest)
        differ = near_vals - far_vals
        gap_value = (
            geometry[:, 0, :] * differ[:, 0, :]
            + geometry[:, 1, :] * differ[:, 1, :]
            + geometry[:, 2, :] * differ[:, 2, :]
            - geometry[:, 3, :]
        )
        depth_value = jnp.where(live_mask, jnp.maximum(-gap_value, 0.0), 0.0)
        contribs = depth_value[:, None, :] * geometry[:, 0:3, :]
        window = jnp.einsum("bcp,bpn->bcn", contribs, near_hot, precision=highest)
        line_hot = (line_index[:, None] == line_ids).astype(jnp.float32)
        running = running + jnp.einsum("bl,bcn->cln", line_hot, window, precision=highest)
        return (running, energy_sum + jnp.sum(depth_value * depth_value))

    initial = (
        jnp.zeros((3, count_lines, near_lines.shape[2]), jnp.float32),
        jnp.zeros((), jnp.float32),
    )
    return lax.fori_loop(0, blocks // group_size, sweep_add_group, initial)


def local(positions, pair_node, pair_line, pair_far, far_line, pair_geom, live_blocks):
    within = pair_node[0, 0, 0]
    line_index = pair_line[0, 0, 0]
    far_pos = pair_far[0, 0, 0]
    far_index = far_line[0, 0, 0]
    geometry = pair_geom[0, 0, 0]
    live_count = live_blocks[0, 0, 0]
    size_x = positions.shape[1]
    size_y = positions.shape[2]
    size_z = positions.shape[3]
    blocks = within.shape[0]
    pair_count = within.shape[1]
    inner_count = blocks // 2
    count_lines = size_x * size_y
    ext_lines = (size_x + 2 * RIM) * (size_y + 2 * RIM)
    ext_z = size_z + 2 * RIM
    devices = lax.axis_size("gx") * lax.axis_size("gy") * lax.axis_size(GZ)
    slot_count = blocks * pair_count
    live_mask = lax.broadcasted_iota(jnp.int32, (blocks, 1), 0) < live_count
    near_hot = (line_index[:, None] == lax.broadcasted_iota(jnp.int32, (1, count_lines), 1)).astype(
        jnp.float32
    )
    far_hot = (far_index[:, None] == lax.broadcasted_iota(jnp.int32, (1, ext_lines), 1)).astype(
        jnp.float32
    )
    live_ones = jnp.broadcast_to(
        jnp.where(live_mask, 1.0, 0.0).astype(jnp.float32), (blocks, pair_count)
    )
    counts = node_sums(live_ones[:, None, :], within, line_index, size_z, count_lines).reshape(
        size_x, size_y, size_z
    )
    widths = ((0, 0), (RIM, RIM), (RIM, RIM), (RIM, RIM))
    padded = extended(positions, (("gx", 1), ("gy", 2), (GZ, 3)), RIM)
    current = positions
    energies = []
    residuals = []
    for sweep_idx in range(SWEEPS):
        near_lines = select_lines(near_hot, current.reshape(3, count_lines, size_z))
        local_pad = jnp.pad(current, widths).reshape(3, ext_lines, ext_z)
        inner_far = select_lines(far_hot[:inner_count], local_pad)
        inner_total, inner_energy = sweep_terms(
            near_lines[:inner_count],
            inner_far,
            within[:inner_count],
            far_pos[:inner_count],
            line_index[:inner_count],
            geometry[:inner_count],
            live_mask[:inner_count],
            count_lines,
        )
        outer_far = select_lines(far_hot[inner_count:], padded.reshape(3, ext_lines, ext_z))
        outer_total, outer_energy = sweep_terms(
            near_lines[inner_count:],
            outer_far,
            within[inner_count:],
            far_pos[inner_count:],
            line_index[inner_count:],
            geometry[inner_count:],
            live_mask[inner_count:],
            count_lines,
        )
        node_total = inner_total + outer_total
        energy_local = inner_energy + outer_energy
        total_energy = one_axis_at_a_time(energy_local, GX_GY_GZ)
        scale_factor = 1.0 / (1.0 + total_energy / (slot_count * devices))
        correction = (
            relax_factor
            * scale_factor
            * node_total.reshape(3, size_x, size_y, size_z)
            / (1.0 + counts)
        )
        current = current + correction
        residual_local = jnp.sum(correction * correction)
        residuals.append(one_axis_at_a_time(residual_local, GX_GY_GZ))
        energies.append(total_energy)
        if sweep_idx + 1 < SWEEPS:
            padded = with_halo(current, (("gx", 1), ("gy", 2), (GZ, 3)), RIM)
    history = jnp.stack(
        [
            jnp.sqrt(1.0 + jnp.stack(energies) / slot_count),
            jnp.sqrt(1.0 + jnp.stack(residuals) / (size_x * size_y * size_z)),
        ]
    )
    return (current, history)


def solution(mesh):
    finer = Mesh(
        mesh.devices.reshape(mesh.shape["gx"], mesh.shape["gy"], 4, 2), ("gx", "gy", "gz_0", "gz_1")
    )
    placed = (
        P(None, "gx", "gy", GZ),
        P("gx", "gy", GZ, None, None),
        P("gx", "gy", GZ, None),
        P("gx", "gy", GZ, None, None),
        P("gx", "gy", GZ, None),
        P("gx", "gy", GZ, None, None, None),
        P("gx", "gy", GZ),
    )
    return jax.shard_map(
        local,
        mesh=finer,
        in_specs=placed,
        out_specs=(P(None, "gx", "gy", GZ), P()),
        check_vma=False,
    )
```

profile of v0, /device:TPU:1, one launch (start us, length us, event | category | flops | bytes accessed | tf_op | source)
XLA Modules:
  0.0 486.6 jit_solution(8755252132308115107)
XLA Ops:
  66.6 8.1 %psum.280 = f32[]{:T(128)} all-reduce(f32[]{:T(128)S(6)} %add.441), channel_id=1, replica_groups=mesh['gx'=4,'gy'=4,'gz_0'=4,'gz_1'=2] {'gx'}, use_global_device_ids=true, to_apply=%region_2.3 | all-reduce | flops 1 | bytes 8 | tf_op jit(solution)/shard_map/psum | solution.py:35
  75.3 10.6 %psum.281 = f32[]{:T(128)} all-reduce(f32[]{:T(128)} %psum.280), channel_id=1, replica_groups=mesh['gx'=4,'gy'=4,'gz_0'=4,'gz_1'=2] {'gy'}, use_global_device_ids=true, to_apply=%region_3.4 | all-reduce | flops 1 | bytes 8 | tf_op jit(solution)/shard_map/psum | solution.py:35
  86.0 7.8 %psum.282 = f32[]{:T(128)} all-reduce(f32[]{:T(128)} %psum.281), channel_id=1, replica_groups=mesh['gx'=4,'gy'=4,'gz_0'=4,'gz_1'=2] {'gz_0'}, use_global_device_ids=true, to_apply=%region_4.5 | all-reduce | flops 1 | bytes 8 | tf_op jit(solution)/shard_map/psum | solution.py:35
  94.7 11.5 %psum.283 = f32[]{:T(128)} all-reduce(f32[]{:T(128)} %psum.282), channel_id=1, replica_groups=mesh['gx'=4,'gy'=4,'gz_0'=4,'gz_1'=2] {'gz_1'}, use_global_device_ids=true, to_apply=%region_5.6 | all-reduce | flops 1 | bytes 8 | tf_op jit(solution)/shard_map/psum | solution.py:35
  154.2 8.4 %psum.284 = f32[]{:T(128)} all-reduce(f32[]{:T(128)S(6)} %add.451), channel_id=1, replica_groups=mesh['gx'=4,'gy'=4,'gz_0'=4,'gz_1'=2] {'gx'}, use_global_device_ids=true, to_apply=%region_10.11 | all-reduce | flops 1 | bytes 8 | tf_op jit(solution)/shard_map/psum | solution.py:35
  162.5 6.6 %psum.285 = f32[]{:T(128)} all-reduce(f32[]{:T(128)} %psum.284), channel_id=1, replica_groups=mesh['gx'=4,'gy'=4,'gz_0'=4,'gz_1'=2] {'gy'}, use_global_device_ids=true, to_apply=%region_11.12 | all-reduce | flops 1 | bytes 8 | tf_op jit(solution)/shard_map/psum | solution.py:35
  170.8 6.6 %psum.286 = f32[]{:T(128)} all-reduce(f32[]{:T(128)} %psum.285), channel_id=1, replica_groups=mesh['gx'=4,'gy'=4,'gz_0'=4,'gz_1'=2] {'gz_0'}, use_global_device_ids=true, to_apply=%region_12.13 | all-reduce | flops 1 | bytes 8 | tf_op jit(solution)/shard_map/psum | solution.py:35
  178.0 9.3 %psum.287 = f32[]{:T(128)} all-reduce(f32[]{:T(128)} %psum.286), channel_id=1, replica_groups=mesh['gx'=4,'gy'=4,'gz_0'=4,'gz_1'=2] {'gz_1'}, use_global_device_ids=true, to_apply=%region_13.14 | all-reduce | flops 1 | bytes 8 | tf_op jit(solution)/shard_map/psum | solution.py:35
  236.3 8.4 %psum.288 = f32[]{:T(128)} all-reduce(f32[]{:T(128)S(6)} %add.459), channel_id=1, replica_groups=mesh['gx'=4,'gy'=4,'gz_0'=4,'gz_1'=2] {'gx'}, use_global_device_ids=true, to_apply=%region_16.17 | all-reduce | flops 1 | bytes 8 | tf_op jit(solution)/shard_map/psum | solution.py:35
  244.7 8.0 %psum.289 = f32[]{:T(128)} all-reduce(f32[]{:T(128)} %psum.288), channel_id=1, replica_groups=mesh['gx'=4,'gy'=4,'gz_0'=4,'gz_1'=2] {'gy'}, use_global_device_ids=true, to_apply=%region_17.18 | all-reduce | flops 1 | bytes 8 | tf_op jit(solution)/shard_map/psum | solution.py:35
  254.4 8.6 %psum.290 = f32[]{:T(128)} all-reduce(f32[]{:T(128)} %psum.289), channel_id=1, replica_groups=mesh['gx'=4,'gy'=4,'gz_0'=4,'gz_1'=2] {'gz_0'}, use_global_device_ids=true, to_apply=%region_18.19 | all-reduce | flops 1 | bytes 8 | tf_op jit(solution)/shard_map/psum | solution.py:35
  263.5 9.0 %psum.291 = f32[]{:T(128)} all-reduce(f32[]{:T(128)} %psum.290), channel_id=1, replica_groups=mesh['gx'=4,'gy'=4,'gz_0'=4,'gz_1'=2] {'gz_1'}, use_global_device_ids=true, to_apply=%region_19.20 | all-reduce | flops 1 | bytes 8 | tf_op jit(solution)/shard_map/psum | solution.py:35
  320.4 8.4 %psum.292 = f32[]{:T(128)} all-reduce(f32[]{:T(128)S(6)} %add.467), channel_id=1, replica_groups=mesh['gx'=4,'gy'=4,'gz_0'=4,'gz_1'=2] {'gx'}, use_global_device_ids=true, to_apply=%region_22.23 | all-reduce | flops 1 | bytes 8 | tf_op jit(solution)/shard_map/psum | solution.py:35
  328.9 6.5 %psum.293 = f32[]{:T(128)} all-reduce(f32[]{:T(128)} %psum.292), channel_id=1, replica_groups=mesh['gx'=4,'gy'=4,'gz_0'=4,'gz_1'=2] {'gy'}, use_global_device_ids=true, to_apply=%region_23.24 | all-reduce | flops 1 | bytes 8 | tf_op jit(solution)/shard_map/psum | solution.py:35
  337.0 6.6 %psum.294 = f32[]{:T(128)} all-reduce(f32[]{:T(128)} %psum.293), channel_id=1, replica_groups=mesh['gx'=4,'gy'=4,'gz_0'=4,'gz_1'=2] {'gz_0'}, use_global_device_ids=true, to_apply=%region_24.25 | all-reduce | flops 1 | bytes 8 | tf_op jit(solution)/shard_map/psum | solution.py:35
  344.2 9.7 %psum.295 = f32[]{:T(128)} all-reduce(f32[]{:T(128)} %psum.294), channel_id=1, replica_groups=mesh['gx'=4,'gy'=4,'gz_0'=4,'gz_1'=2] {'gz_1'}, use_global_device_ids=true, to_apply=%region_25.26 | all-reduce | flops 1 | bytes 8 | tf_op jit(solution)/shard_map/psum | solution.py:35
  406.6 8.3 %psum.296 = f32[]{:T(128)} all-reduce(f32[]{:T(128)S(6)} %add.475), channel_id=1, replica_groups=mesh['gx'=4,'gy'=4,'gz_0'=4,'gz_1'=2] {'gx'}, use_global_device_ids=true, to_apply=%region_28.29 | all-reduce | flops 1 | bytes 8 | tf_op jit(solution)/shard_map/psum | solution.py:35
  417.3 7.9 %psum.297 = f32[]{:T(128)} all-reduce(f32[]{:T(128)} %psum.296), channel_id=1, replica_groups=mesh['gx'=4,'gy'=4,'gz_0'=4,'gz_1'=2] {'gy'}, use_global_device_ids=true, to_apply=%region_29.30 | all-reduce | flops 1 | bytes 8 | tf_op jit(solution)/shard_map/psum | solution.py:35
  425.1 8.2 %psum.298 = f32[]{:T(128)} all-reduce(f32[]{:T(128)} %psum.297), channel_id=1, replica_groups=mesh['gx'=4,'gy'=4,'gz_0'=4,'gz_1'=2] {'gz_0'}, use_global_device_ids=true, to_apply=%region_30.31 | all-reduce | flops 1 | bytes 8 | tf_op jit(solution)/shard_map/psum | solution.py:35
  435.6 9.4 %psum.299 = f32[]{:T(128)} all-reduce(f32[]{:T(128)} %psum.298), channel_id=1, replica_groups=mesh['gx'=4,'gy'=4,'gz_0'=4,'gz_1'=2] {'gz_1'}, use_global_device_ids=true, to_apply=%region_31.32 | all-reduce | flops 1 | bytes 8 | tf_op jit(solution)/shard_map/psum | solution.py:35
  449.9 6.8 %all-reduce.23 = (f32[]{:T(128)}, f32[]{:T(128)}, f32[]{:T(128)}, f32[]{:T(128)}, f32[]{:T(128)}) all-reduce(f32[]{:T(128)} %get-tuple-element.530, f32[]{:T(128)} %get-tuple-element.527, f32[]{:T(128)} %get-tuple-element.528, f32[]{:T(128)} %get-tuple-element.529, ...), channel_id=1, replica_groups=mesh['gx'=4,'gy'=4,'gz_0'=4,'gz_1'=2] {'gx'}, use_global_device_ids=true, to_apply=%region_33.34 | all-reduce | flops 5 | bytes 40 | tf_op jit(solution)/shard_map/psum | solution.py:35
  456.7 7.0 %all-reduce.22 = (f32[]{:T(128)}, f32[]{:T(128)}, f32[]{:T(128)}, f32[]{:T(128)}, f32[]{:T(128)}) all-reduce(f32[]{:T(128)} %get-tuple-element.564, f32[]{:T(128)} %get-tuple-element.565, f32[]{:T(128)} %get-tuple-element.566, f32[]{:T(128)} %get-tuple-element.567, ...), channel_id=1, replica_groups=mesh['gx'=4,'gy'=4,'gz_0'=4,'gz_1'=2] {'gy'}, use_global_device_ids=true, to_apply=%region_34.35 | all-reduce | flops 5 | bytes 40 | tf_op jit(solution)/shard_map/psum | solution.py:35
  463.7 6.7 %all-reduce.21 = (f32[]{:T(128)}, f32[]{:T(128)}, f32[]{:T(128)}, f32[]{:T(128)}, f32[]{:T(128)}) all-reduce(f32[]{:T(128)} %get-tuple-element.559, f32[]{:T(128)} %get-tuple-element.560, f32[]{:T(128)} %get-tuple-element.561, f32[]{:T(128)} %get-tuple-element.562, ...), channel_id=1, replica_groups=mesh['gx'=4,'gy'=4,'gz_0'=4,'gz_1'=2] {'gz_0'}, use_global_device_ids=true, to_apply=%region_35.36 | all-reduce | flops 5 | bytes 40 | tf_op jit(solution)/shard_map/psum | solution.py:35
  470.4 8.6 %all-reduce.24 = (f32[1,1]{1,0:T(1,128)}, f32[1,1]{1,0:T(1,128)}, f32[1,1]{1,0:T(1,128)}, f32[1,1]{1,0:T(1,128)}, f32[1,1]{1,0:T(1,128)}) all-reduce(f32[1,1]{1,0:T(1,128)} %bitcast.57, f32[1,1]{1,0:T(1,128)} %bitcast.58, f32[1,1]{1,0:T(1,128)} %bitcast.59, ...), channel_id=1, replica_groups=mesh['gx'=4,'gy'=4,'gz_0'=4,'gz_1'=2] {'gz_1'}, use_global_device_ids=true, to_apply=%region_36.37 | all-reduce | flops 5 | bytes 40 | tf_op jit(solution)/shard_map/psum | solution.py:35
  (344 shorter events, 281.1 us)
Async XLA Ops:
  2.4 27.4 %collective-permute-start.1 = (f32[3,3,16,256]{3,1,2,0:T(4,128)S(1)}, f32[3,3,16,256]{3,1,2,0:T(4,128)S(1)}, u32[]{:S(2)}, u32[]{:S(2)}) collective-permute-start(f32[3,3,16,256]{3,1,2,0:T(4,128)S(1)} %get-tuple-element.629), channel_id=1, source_target_pairs={{32,0},{64,32},{96,64},{33,1},{65,33},{97,65},{34,2},{66,34},{98,6... | collective-permute-start | bytes 442376 | tf_op jit(solution)/shard_map/ppermute | solution.py:26
  3.7 26.1 %collective-permute-start = (f32[3,3,16,256]{3,1,2,0:T(4,128)S(1)}, f32[3,3,16,256]{3,1,2,0:T(4,128)S(1)}, u32[]{:S(2)}, u32[]{:S(2)}) collective-permute-start(f32[3,3,16,256]{3,1,2,0:T(4,128)S(1)} %get-tuple-element.628), channel_id=1, source_target_pairs={{0,32},{32,64},{64,96},{1,33},{33,65},{65,97},{2,34},{34,66},{66,9... | collective-permute-start | bytes 442376 | tf_op jit(solution)/shard_map/ppermute | solution.py:24
  29.9 8.1 %collective-permute-start.3 = (f32[3,22,3,256]{3,1,2,0:T(8,128)S(1)}, f32[3,22,3,256]{3,1,2,0:T(8,128)S(1)}, u32[]{:S(2)}, u32[]{:S(2)}) collective-permute-start(f32[3,22,3,256]{3,1,2,0:T(8,128)S(1)} %get-tuple-element.595), channel_id=1, source_target_pairs={{8,0},{16,8},{24,16},{9,1},{17,9},{25,17},{10,2},{18,10},{26,18},{... | collective-permute-start | bytes 608264 | tf_op jit(solution)/shard_map/ppermute | solution.py:26
  43.1 9.6 %collective-permute-start.5 = (f32[3,22,22,3]{2,1,3,0:T(8,128)S(1)}, f32[3,22,22,3]{2,1,3,0:T(8,128)S(1)}, u32[]{:S(2)}, u32[]{:S(2)}) collective-permute-start(f32[3,22,22,3]{2,1,3,0:T(8,128)S(1)} %copy.135), channel_id=1, source_target_pairs={{1,0},{2,1},{3,2},{4,3},{5,4},{6,5},{7,6},{9,8},{10,9},{11,10},{12... | collective-permute-start | bytes 52280 | tf_op jit(solution)/shard_map/ppermute | solution.py:26
  110.0 15.3 %collective-permute-start.11 = (f32[3,16,16,3]{3,2,1,0:T(8,128)S(1)}, f32[3,16,16,3]{3,2,1,0:T(8,128)S(1)}, u32[]{:S(2)}, u32[]{:S(2)}) collective-permute-start(f32[3,16,16,3]{3,2,1,0:T(8,128)S(1)} %get-tuple-element.625), channel_id=1, source_target_pairs={{1,0},{2,1},{3,2},{4,3},{5,4},{6,5},{7,6},{9,8},{10,9},{11,10},{12... | collective-permute-start | bytes 27656 | tf_op jit(solution)/shard_map/ppermute | solution.py:48
  112.3 19.6 %collective-permute-start.10 = (f32[3,16,3,256]{3,2,1,0:T(4,128)S(1)}, f32[3,16,3,256]{3,2,1,0:T(4,128)S(1)}, u32[]{:S(2)}, u32[]{:S(2)}) collective-permute-start(f32[3,16,3,256]{3,2,1,0:T(4,128)S(1)} %get-tuple-element.627), channel_id=1, source_target_pairs={{8,0},{16,8},{24,16},{9,1},{17,9},{25,17},{10,2},{18,10},{26,18},{... | collective-permute-start | bytes 442376 | tf_op jit(solution)/shard_map/ppermute | solution.py:48
  113.6 18.4 %collective-permute-start.7 = (f32[3,16,3,256]{3,2,1,0:T(4,128)S(1)}, f32[3,16,3,256]{3,2,1,0:T(4,128)S(1)}, u32[]{:S(2)}, u32[]{:S(2)}) collective-permute-start(f32[3,16,3,256]{3,2,1,0:T(4,128)S(1)} %get-tuple-element.626), channel_id=1, source_target_pairs={{0,8},{8,16},{16,24},{1,9},{9,17},{17,25},{2,10},{10,18},{18,26},{... | collective-permute-start | bytes 442376 | tf_op jit(solution)/shard_map/ppermute | solution.py:47
  117.6 14.3 %collective-permute-start.6 = (f32[3,16,16,3]{3,2,1,0:T(8,128)S(1)}, f32[3,16,16,3]{3,2,1,0:T(8,128)S(1)}, u32[]{:S(2)}, u32[]{:S(2)}) collective-permute-start(f32[3,16,16,3]{3,2,1,0:T(8,128)S(1)} %get-tuple-element.624), channel_id=1, source_target_pairs={{0,1},{1,2},{2,3},{3,4},{4,5},{5,6},{6,7},{8,9},{9,10},{10,11},{11... | collective-permute-start | bytes 27656 | tf_op jit(solution)/shard_map/ppermute | solution.py:47
  121.4 10.5 %collective-permute-start.9 = (f32[3,3,16,256]{3,2,1,0:T(8,128)S(1)}, f32[3,3,16,256]{3,2,1,0:T(8,128)S(1)}, u32[]{:S(2)}, u32[]{:S(2)}) collective-permute-start(f32[3,3,16,256]{3,2,1,0:T(8,128)S(1)} %get-tuple-element.623), channel_id=1, source_target_pairs={{32,0},{64,32},{96,64},{33,1},{65,33},{97,65},{34,2},{66,34},{98,6... | collective-permute-start | bytes 442376 | tf_op jit(solution)/shard_map/ppermute | solution.py:48
  191.1 16.0 %collective-permute-start.17 = (f32[3,16,16,3]{3,2,1,0:T(8,128)S(1)}, f32[3,16,16,3]{3,2,1,0:T(8,128)S(1)}, u32[]{:S(2)}, u32[]{:S(2)}) collective-permute-start(f32[3,16,16,3]{3,2,1,0:T(8,128)S(1)} %get-tuple-element.617), channel_id=1, source_target_pairs={{1,0},{2,1},{3,2},{4,3},{5,4},{6,5},{7,6},{9,8},{10,9},{11,10},{12... | collective-permute-start | bytes 27656 | tf_op jit(solution)/shard_map/ppermute | solution.py:48
  193.4 20.6 %collective-permute-start.16 = (f32[3,16,3,256]{3,2,1,0:T(4,128)S(1)}, f32[3,16,3,256]{3,2,1,0:T(4,128)S(1)}, u32[]{:S(2)}, u32[]{:S(2)}) collective-permute-start(f32[3,16,3,256]{3,2,1,0:T(4,128)S(1)} %get-tuple-element.619), channel_id=1, source_target_pairs={{8,0},{16,8},{24,16},{9,1},{17,9},{25,17},{10,2},{18,10},{26,18},{... | collective-permute-start | bytes 442376 | tf_op jit(solution)/shard_map/ppermute | solution.py:48
  194.7 19.4 %collective-permute-start.13 = (f32[3,16,3,256]{3,2,1,0:T(4,128)S(1)}, f32[3,16,3,256]{3,2,1,0:T(4,128)S(1)}, u32[]{:S(2)}, u32[]{:S(2)}) collective-permute-start(f32[3,16,3,256]{3,2,1,0:T(4,128)S(1)} %get-tuple-element.618), channel_id=1, source_target_pairs={{0,8},{8,16},{16,24},{1,9},{9,17},{17,25},{2,10},{10,18},{18,26},{... | collective-permute-start | bytes 442376 | tf_op jit(solution)/shard_map/ppermute | solution.py:47
  198.9 15.1 %collective-permute-start.12 = (f32[3,16,16,3]{3,2,1,0:T(8,128)S(1)}, f32[3,16,16,3]{3,2,1,0:T(8,128)S(1)}, u32[]{:S(2)}, u32[]{:S(2)}) collective-permute-start(f32[3,16,16,3]{3,2,1,0:T(8,128)S(1)} %get-tuple-element.616), channel_id=1, source_target_pairs={{0,1},{1,2},{2,3},{3,4},{4,5},{5,6},{6,7},{8,9},{9,10},{10,11},{11... | collective-permute-start | bytes 27656 | tf_op jit(solution)/shard_map/ppermute | solution.py:47
  202.5 11.5 %collective-permute-start.15 = (f32[3,3,16,256]{3,2,1,0:T(8,128)S(1)}, f32[3,3,16,256]{3,2,1,0:T(8,128)S(1)}, u32[]{:S(2)}, u32[]{:S(2)}) collective-permute-start(f32[3,3,16,256]{3,2,1,0:T(8,128)S(1)} %get-tuple-element.615), channel_id=1, source_target_pairs={{32,0},{64,32},{96,64},{33,1},{65,33},{97,65},{34,2},{66,34},{98,6... | collective-permute-start | bytes 442376 | tf_op jit(solution)/shard_map/ppermute | solution.py:48
  276.4 15.3 %collective-permute-start.23 = (f32[3,16,16,3]{3,2,1,0:T(8,128)S(1)}, f32[3,16,16,3]{3,2,1,0:T(8,128)S(1)}, u32[]{:S(2)}, u32[]{:S(2)}) collective-permute-start(f32[3,16,16,3]{3,2,1,0:T(8,128)S(1)} %get-tuple-element.609), channel_id=1, source_target_pairs={{1,0},{2,1},{3,2},{4,3},{5,4},{6,5},{7,6},{9,8},{10,9},{11,10},{12... | collective-permute-start | bytes 27656 | tf_op jit(solution)/shard_map/ppermute | solution.py:48
  278.7 19.5 %collective-permute-start.22 = (f32[3,16,3,256]{3,2,1,0:T(4,128)S(1)}, f32[3,16,3,256]{3,2,1,0:T(4,128)S(1)}, u32[]{:S(2)}, u32[]{:S(2)}) collective-permute-start(f32[3,16,3,256]{3,2,1,0:T(4,128)S(1)} %get-tuple-element.611), channel_id=1, source_target_pairs={{8,0},{16,8},{24,16},{9,1},{17,9},{25,17},{10,2},{18,10},{26,18},{... | collective-permute-start | bytes 442376 | tf_op jit(solution)/shard_map/ppermute | solution.py:48
  280.0 18.2 %collective-permute-start.19 = (f32[3,16,3,256]{3,2,1,0:T(4,128)S(1)}, f32[3,16,3,256]{3,2,1,0:T(4,128)S(1)}, u32[]{:S(2)}, u32[]{:S(2)}) collective-permute-start(f32[3,16,3,256]{3,2,1,0:T(4,128)S(1)} %get-tuple-element.610), channel_id=1, source_target_pairs={{0,8},{8,16},{16,24},{1,9},{9,17},{17,25},{2,10},{10,18},{18,26},{... | collective-permute-start | bytes 442376 | tf_op jit(solution)/shard_map/ppermute | solution.py:47
  284.0 14.1 %collective-permute-start.18 = (f32[3,16,16,3]{3,2,1,0:T(8,128)S(1)}, f32[3,16,16,3]{3,2,1,0:T(8,128)S(1)}, u32[]{:S(2)}, u32[]{:S(2)}) collective-permute-start(f32[3,16,16,3]{3,2,1,0:T(8,128)S(1)} %get-tuple-element.608), channel_id=1, source_target_pairs={{0,1},{1,2},{2,3},{3,4},{4,5},{5,6},{6,7},{8,9},{9,10},{10,11},{11... | collective-permute-start | bytes 27656 | tf_op jit(solution)/shard_map/ppermute | solution.py:47
  287.9 10.3 %collective-permute-start.21 = (f32[3,3,16,256]{3,2,1,0:T(8,128)S(1)}, f32[3,3,16,256]{3,2,1,0:T(8,128)S(1)}, u32[]{:S(2)}, u32[]{:S(2)}) collective-permute-start(f32[3,3,16,256]{3,2,1,0:T(8,128)S(1)} %get-tuple-element.607), channel_id=1, source_target_pairs={{32,0},{64,32},{96,64},{33,1},{65,33},{97,65},{34,2},{66,34},{98,6... | collective-permute-start | bytes 442376 | tf_op jit(solution)/shard_map/ppermute | solution.py:48
  357.8 16.0 %collective-permute-start.29 = (f32[3,16,16,3]{3,2,1,0:T(8,128)S(1)}, f32[3,16,16,3]{3,2,1,0:T(8,128)S(1)}, u32[]{:S(2)}, u32[]{:S(2)}) collective-permute-start(f32[3,16,16,3]{3,2,1,0:T(8,128)S(1)} %get-tuple-element.601), channel_id=1, source_target_pairs={{1,0},{2,1},{3,2},{4,3},{5,4},{6,5},{7,6},{9,8},{10,9},{11,10},{12... | collective-permute-start | bytes 27656 | tf_op jit(solution)/shard_map/ppermute | solution.py:48
  360.0 20.7 %collective-permute-start.28 = (f32[3,16,3,256]{3,2,1,0:T(4,128)S(1)}, f32[3,16,3,256]{3,2,1,0:T(4,128)S(1)}, u32[]{:S(2)}, u32[]{:S(2)}) collective-permute-start(f32[3,16,3,256]{3,2,1,0:T(4,128)S(1)} %get-tuple-element.603), channel_id=1, source_target_pairs={{8,0},{16,8},{24,16},{9,1},{17,9},{25,17},{10,2},{18,10},{26,18},{... | collective-permute-start | bytes 442376 | tf_op jit(solution)/shard_map/ppermute | solution.py:48
  361.3 19.4 %collective-permute-start.25 = (f32[3,16,3,256]{3,2,1,0:T(4,128)S(1)}, f32[3,16,3,256]{3,2,1,0:T(4,128)S(1)}, u32[]{:S(2)}, u32[]{:S(2)}) collective-permute-start(f32[3,16,3,256]{3,2,1,0:T(4,128)S(1)} %get-tuple-element.602), channel_id=1, source_target_pairs={{0,8},{8,16},{16,24},{1,9},{9,17},{17,25},{2,10},{10,18},{18,26},{... | collective-permute-start | bytes 442376 | tf_op jit(solution)/shard_map/ppermute | solution.py:47
  365.3 15.4 %collective-permute-start.24 = (f32[3,16,16,3]{3,2,1,0:T(8,128)S(1)}, f32[3,16,16,3]{3,2,1,0:T(8,128)S(1)}, u32[]{:S(2)}, u32[]{:S(2)}) collective-permute-start(f32[3,16,16,3]{3,2,1,0:T(8,128)S(1)} %get-tuple-element.600), channel_id=1, source_target_pairs={{0,1},{1,2},{2,3},{3,4},{4,5},{5,6},{6,7},{8,9},{9,10},{10,11},{11... | collective-permute-start | bytes 27656 | tf_op jit(solution)/shard_map/ppermute | solution.py:47
  369.2 11.6 %collective-permute-start.27 = (f32[3,3,16,256]{3,2,1,0:T(8,128)S(1)}, f32[3,3,16,256]{3,2,1,0:T(8,128)S(1)}, u32[]{:S(2)}, u32[]{:S(2)}) collective-permute-start(f32[3,3,16,256]{3,2,1,0:T(8,128)S(1)} %get-tuple-element.599), channel_id=1, source_target_pairs={{32,0},{64,32},{96,64},{33,1},{65,33},{97,65},{34,2},{66,34},{98,6... | collective-permute-start | bytes 442376 | tf_op jit(solution)/shard_map/ppermute | solution.py:48
  (61 other events, 916.9 us)
where the time goes:
time: 496 us; the launch traced here: 487 us
  blocking collectives  197 us (40%)
  matrix products  104 us (21%)
  starting transfers between devices  86.6 us (17%)
  local copies, waits for them, and re-layouts  48.9 us (10%)
  other arithmetic  35.3 us (7%)
  between operations  12.6 us (3%)
    psum x24, blocking collectives, one_axis_at_a_time(): x = lax.psum(x, axis)  197 us
    ppermute x12, starting transfers between devices, with_halo(): lax.ppermute(last, axis, up)  48.5 us
    dot_general x15, matrix products, select_lines(): return jnp.einsum('bl,cln->bcn', line_hot, field_lines, precision=highest)  27.1 us
    dot_general x10, matrix products, sweep_add_group(): jnp.einsum('bcn,bpn->bcp', near_lines, near_hot, precision=highest)  24.6 us
    ppermute x12, starting transfers between devices, with_halo(): lax.ppermute(first, axis, [(b, a) for a, b in up])  19.3 us
    dot_general x10, matrix products, sweep_add_group(): far_vals = jnp.einsum('bcn,bpn->bcp', far_lines, far_hot, precision=highest)  19.3 us
    dot_general x10, matrix products, sweep_add_group(): window = jnp.einsum('bcp,bpn->bcn', contribs, near_hot, precision=highest)  18.6 us
    concatenate x4, other arithmetic, with_halo(): jnp.concatenate([jnp.pad(low, around), x, jnp.pad(high, around)], axis=dim)  18.4 us
  transfers between devices with their start and end apart: 30, of which 5 were waited for; matrix products, arithmetic and copies ran while one was open for 10% of the time, Pallas kernels for 0%

commit v1 on v0

--- a/solution.py
+++ b/solution.py
@@ -32,7 +32,8 @@
 
 def one_axis_at_a_time(x, axes):
     for axis in axes:
-        x = lax.psum(x, axis)
+        clean = jax.lax.all_gather(x, axis)
+        x = jnp.sum(clean, 0)
     return x
 
 

time: 496 us -> 561 us (1.13)
  local copies, waits for them, and re-layouts: 48.9 us -> 101 us
  other arithmetic: 35.3 us -> 60.6 us
  blocking collectives: 197 us -> 182 us
    psum x24 -> x0, blocking collectives: 197 us -> none  [one_axis_at_a_time(): x = lax.psum(x, axis)]
    unnamed x0 -> x24, blocking collectives: none -> 182 us
    unnamed x113 -> x223, local copies, waits for them, and re-layouts: 3.97 us -> 56.2 us
    reduce_sum x0 -> x40, other arithmetic: none -> 24.2 us  [one_axis_at_a_time(): x = jnp.sum(clean, 0)]
  transfers between devices with their start and end apart: 30 -> 30, of which waited for: 5 -> 5; matrix products, arithmetic and copies ran while one was open for 10% -> 9% of each run, Pallas kernels for 0% -> 0%
where the time goes in v1:
time: 561 us; the launch traced here: 551 us
  blocking collectives  182 us (32%)
  matrix products  106 us (19%)
  local copies, waits for them, and re-layouts  101 us (18%)
  starting transfers between devices  86.2 us (15%)
  other arithmetic  60.6 us (11%)
  between operations  12.6 us (2%)
    unnamed x24, blocking collectives  182 us
    unnamed x223, local copies, waits for them, and re-layouts  56.2 us
    ppermute x12, starting transfers between devices, with_halo(): lax.ppermute(last, axis, up)  47.6 us
    dot_general x15, matrix products, select_lines(): return jnp.einsum('bl,cln->bcn', line_hot, field_lines, precision=highest)  27.2 us
    dot_general x10, matrix products, sweep_add_group(): jnp.einsum('bcn,bpn->bcp', near_lines, near_hot, precision=highest)  25.2 us
    reduce_sum x40, other arithmetic, one_axis_at_a_time(): x = jnp.sum(clean, 0)  24.2 us
    ppermute x12, starting transfers between devices, with_halo(): lax.ppermute(first, axis, [(b, a) for a, b in up])  19.6 us
    dot_general x10, matrix products, sweep_add_group(): far_vals = jnp.einsum('bcn,bpn->bcp', far_lines, far_hot, precision=highest)  19.3 us
  transfers between devices with their start and end apart: 30, of which 5 were waited for; matrix products, arithmetic and copies ran while one was open for 9% of the time, Pallas kernels for 0%

profile of v1, /device:TPU:1, one launch (start us, length us, event | category | flops | bytes accessed | tf_op | source)
XLA Modules:
  0.0 551.0 jit_solution(2219014813112868592)
XLA Ops:
  70.8 7.6 %all-reduce.21 = f32[4]{0:T(128)S(1)} all-reduce(f32[4]{0:T(128)S(1)} %dynamic-update-slice), channel_id=1, replica_groups=mesh['gx'=4,'gy'=4,'gz_0'=4,'gz_1'=2] {'gx'}, use_global_device_ids=true, to_apply=%add.21 | all-reduce | flops 4 | bytes 32
  81.0 9.9 %all-reduce.22 = f32[4]{0:T(128)S(1)} all-reduce(f32[4]{0:T(128)S(1)} %dynamic-update-slice.1), channel_id=1, replica_groups=mesh['gx'=4,'gy'=4,'gz_0'=4,'gz_1'=2] {'gy'}, use_global_device_ids=true, to_apply=%add.22 | all-reduce | flops 4 | bytes 32
  93.4 7.3 %all-reduce.23 = f32[4]{0:T(128)S(1)} all-reduce(f32[4]{0:T(128)S(1)} %dynamic-update-slice.2), channel_id=1, replica_groups=mesh['gx'=4,'gy'=4,'gz_0'=4,'gz_1'=2] {'gz_0'}, use_global_device_ids=true, to_apply=%add.23 | all-reduce | flops 4 | bytes 32
  102.7 10.2 %all-reduce.24 = f32[2]{0:T(128)S(1)} all-reduce(f32[2]{0:T(128)S(1)} %dynamic-update-slice.3), channel_id=1, replica_groups=mesh['gx'=4,'gy'=4,'gz_0'=4,'gz_1'=2] {'gz_1'}, use_global_device_ids=true, to_apply=%add.24 | all-reduce | flops 2 | bytes 16
  162.2 7.9 %all-reduce.25 = f32[4]{0:T(128)S(1)} all-reduce(f32[4]{0:T(128)S(1)} %dynamic-update-slice.4), channel_id=1, replica_groups=mesh['gx'=4,'gy'=4,'gz_0'=4,'gz_1'=2] {'gx'}, use_global_device_ids=true, to_apply=%add.25 | all-reduce | flops 4 | bytes 32
  172.2 6.0 %all-reduce.26 = f32[4]{0:T(128)S(1)} all-reduce(f32[4]{0:T(128)S(1)} %dynamic-update-slice.5), channel_id=1, replica_groups=mesh['gx'=4,'gy'=4,'gz_0'=4,'gz_1'=2] {'gy'}, use_global_device_ids=true, to_apply=%add.26 | all-reduce | flops 4 | bytes 32
  181.7 6.0 %all-reduce.27 = f32[4]{0:T(128)S(1)} all-reduce(f32[4]{0:T(128)S(1)} %dynamic-update-slice.6), channel_id=1, replica_groups=mesh['gx'=4,'gy'=4,'gz_0'=4,'gz_1'=2] {'gz_0'}, use_global_device_ids=true, to_apply=%add.27 | all-reduce | flops 4 | bytes 32
  190.2 8.6 %all-reduce.28 = f32[2]{0:T(128)S(1)} all-reduce(f32[2]{0:T(128)S(1)} %dynamic-update-slice.7), channel_id=1, replica_groups=mesh['gx'=4,'gy'=4,'gz_0'=4,'gz_1'=2] {'gz_1'}, use_global_device_ids=true, to_apply=%add.28 | all-reduce | flops 2 | bytes 16
  249.5 7.9 %all-reduce.29 = f32[4]{0:T(128)S(1)} all-reduce(f32[4]{0:T(128)S(1)} %dynamic-update-slice.8), channel_id=1, replica_groups=mesh['gx'=4,'gy'=4,'gz_0'=4,'gz_1'=2] {'gx'}, use_global_device_ids=true, to_apply=%add.29 | all-reduce | flops 4 | bytes 32
  259.5 7.4 %all-reduce.30 = f32[4]{0:T(128)S(1)} all-reduce(f32[4]{0:T(128)S(1)} %dynamic-update-slice.9), channel_id=1, replica_groups=mesh['gx'=4,'gy'=4,'gz_0'=4,'gz_1'=2] {'gy'}, use_global_device_ids=true, to_apply=%add.30 | all-reduce | flops 4 | bytes 32
  270.4 7.9 %all-reduce.31 = f32[4]{0:T(128)S(1)} all-reduce(f32[4]{0:T(128)S(1)} %dynamic-update-slice.10), channel_id=1, replica_groups=mesh['gx'=4,'gy'=4,'gz_0'=4,'gz_1'=2] {'gz_0'}, use_global_device_ids=true, to_apply=%add.31 | all-reduce | flops 4 | bytes 32
  280.9 8.8 %all-reduce.32 = f32[2]{0:T(128)S(1)} all-reduce(f32[2]{0:T(128)S(1)} %dynamic-update-slice.11), channel_id=1, replica_groups=mesh['gx'=4,'gy'=4,'gz_0'=4,'gz_1'=2] {'gz_1'}, use_global_device_ids=true, to_apply=%add.32 | all-reduce | flops 2 | bytes 16
  339.6 7.9 %all-reduce.33 = f32[4]{0:T(128)S(1)} all-reduce(f32[4]{0:T(128)S(1)} %dynamic-update-slice.12), channel_id=1, replica_groups=mesh['gx'=4,'gy'=4,'gz_0'=4,'gz_1'=2] {'gx'}, use_global_device_ids=true, to_apply=%add.33 | all-reduce | flops 4 | bytes 32
  349.7 6.0 %all-reduce.34 = f32[4]{0:T(128)S(1)} all-reduce(f32[4]{0:T(128)S(1)} %dynamic-update-slice.13), channel_id=1, replica_groups=mesh['gx'=4,'gy'=4,'gz_0'=4,'gz_1'=2] {'gy'}, use_global_device_ids=true, to_apply=%add.34 | all-reduce | flops 4 | bytes 32
  359.3 6.2 %all-reduce.35 = f32[4]{0:T(128)S(1)} all-reduce(f32[4]{0:T(128)S(1)} %dynamic-update-slice.14), channel_id=1, replica_groups=mesh['gx'=4,'gy'=4,'gz_0'=4,'gz_1'=2] {'gz_0'}, use_global_device_ids=true, to_apply=%add.35 | all-reduce | flops 4 | bytes 32
  368.2 9.2 %all-reduce.36 = f32[2]{0:T(128)S(1)} all-reduce(f32[2]{0:T(128)S(1)} %dynamic-update-slice.15), channel_id=1, replica_groups=mesh['gx'=4,'gy'=4,'gz_0'=4,'gz_1'=2] {'gz_1'}, use_global_device_ids=true, to_apply=%add.36 | all-reduce | flops 2 | bytes 16
  431.3 7.9 %all-reduce.37 = f32[4]{0:T(128)S(1)} all-reduce(f32[4]{0:T(128)S(1)} %dynamic-update-slice.16), channel_id=1, replica_groups=mesh['gx'=4,'gy'=4,'gz_0'=4,'gz_1'=2] {'gx'}, use_global_device_ids=true, to_apply=%add.37 | all-reduce | flops 4 | bytes 32
  443.4 7.1 %all-reduce.38 = f32[4]{0:T(128)S(1)} all-reduce(f32[4]{0:T(128)S(1)} %dynamic-update-slice.17), channel_id=1, replica_groups=mesh['gx'=4,'gy'=4,'gz_0'=4,'gz_1'=2] {'gy'}, use_global_device_ids=true, to_apply=%add.38 | all-reduce | flops 4 | bytes 32
  452.4 7.6 %all-reduce.39 = f32[4]{0:T(128)S(1)} all-reduce(f32[4]{0:T(128)S(1)} %dynamic-update-slice.18), channel_id=1, replica_groups=mesh['gx'=4,'gy'=4,'gz_0'=4,'gz_1'=2] {'gz_0'}, use_global_device_ids=true, to_apply=%add.39 | all-reduce | flops 4 | bytes 32
  464.2 8.7 %all-reduce.40 = f32[2]{0:T(128)S(1)} all-reduce(f32[2]{0:T(128)S(1)} %dynamic-update-slice.19), channel_id=1, replica_groups=mesh['gx'=4,'gy'=4,'gz_0'=4,'gz_1'=2] {'gz_1'}, use_global_device_ids=true, to_apply=%add.40 | all-reduce | flops 2 | bytes 16
  484.6 6.1 %all-reduce.63 = (f32[4]{0:T(128)S(1)}, f32[4]{0:T(128)S(1)}, f32[4]{0:T(128)S(1)}, f32[4]{0:T(128)S(1)}, f32[4]{0:T(128)S(1)}) all-reduce(f32[4]{0:T(128)S(1)} %dynamic-update-slice.20, f32[4]{0:T(128)S(1)} %dynamic-update-slice.24, f32[4]{0:T(128)S(1)} %dynamic-update-slice.28, ...), channel_id=1, replica_groups=mesh['gx'=4,'gy'=4,'gz_0'=4,'gz_1'=2] {'gx'}, use_global_device_ids=true, to_apply=%add.41 | all-reduce | flops 20 | bytes 160
  500.4 6.3 %all-reduce.62 = (f32[4]{0:T(128)S(1)}, f32[4]{0:T(128)S(1)}, f32[4]{0:T(128)S(1)}, f32[4]{0:T(128)S(1)}, f32[4]{0:T(128)S(1)}) all-reduce(f32[4]{0:T(128)S(1)} %dynamic-update-slice.21, f32[4]{0:T(128)S(1)} %dynamic-update-slice.25, f32[4]{0:T(128)S(1)} %dynamic-update-slice.29, ...), channel_id=1, replica_groups=mesh['gx'=4,'gy'=4,'gz_0'=4,'gz_1'=2] {'gy'}, use_global_device_ids=true, to_apply=%add.42 | all-reduce | flops 20 | bytes 160
  515.7 6.0 %all-reduce.61 = (f32[4]{0:T(128)S(1)}, f32[4]{0:T(128)S(1)}, f32[4]{0:T(128)S(1)}, f32[4]{0:T(128)S(1)}, f32[4]{0:T(128)S(1)}) all-reduce(f32[4]{0:T(128)S(1)} %dynamic-update-slice.22, f32[4]{0:T(128)S(1)} %dynamic-update-slice.26, f32[4]{0:T(128)S(1)} %dynamic-update-slice.30, ...), channel_id=1, replica_groups=mesh['gx'=4,'gy'=4,'gz_0'=4,'gz_1'=2] {'gz_0'}, use_global_device_ids=true, to_apply=%add.43 | all-reduce | flops 20 | bytes 160
  533.0 7.9 %all-reduce.64 = (f32[2]{0:T(128)S(1)}, f32[2]{0:T(128)S(1)}, f32[2]{0:T(128)S(1)}, f32[2]{0:T(128)S(1)}, f32[2]{0:T(128)S(1)}) all-reduce(f32[2]{0:T(128)S(1)} %dynamic-update-slice.23, f32[2]{0:T(128)S(1)} %dynamic-update-slice.27, f32[2]{0:T(128)S(1)} %dynamic-update-slice.31, ...), channel_id=1, replica_groups=mesh['gx'=4,'gy'=4,'gz_0'=4,'gz_1'=2] {'gz_1'}, use_global_device_ids=true, to_apply=%add.44 | all-reduce | flops 10 | bytes 80
  (494 shorter events, 360.6 us)
Async XLA Ops:
  2.4 29.3 %collective-permute-start.1 = (f32[3,3,16,256]{3,1,2,0:T(4,128)S(1)}, f32[3,3,16,256]{3,1,2,0:T(4,128)S(1)}, u32[]{:S(2)}, u32[]{:S(2)}) collective-permute-start(f32[3,3,16,256]{3,1,2,0:T(4,128)S(1)} %get-tuple-element.629), channel_id=1, source_target_pairs={{32,0},{64,32},{96,64},{33,1},{65,33},{97,65},{34,2},{66,34},{98,6... | collective-permute-start | bytes 442376 | tf_op jit(solution)/shard_map/ppermute | solution.py:26
  3.7 28.0 %collective-permute-start = (f32[3,3,16,256]{3,1,2,0:T(4,128)S(1)}, f32[3,3,16,256]{3,1,2,0:T(4,128)S(1)}, u32[]{:S(2)}, u32[]{:S(2)}) collective-permute-start(f32[3,3,16,256]{3,1,2,0:T(4,128)S(1)} %get-tuple-element.628), channel_id=1, source_target_pairs={{0,32},{32,64},{64,96},{1,33},{33,65},{65,97},{2,34},{34,66},{66,9... | collective-permute-start | bytes 442376 | tf_op jit(solution)/shard_map/ppermute | solution.py:24
  31.8 8.1 %collective-permute-start.3 = (f32[3,22,3,256]{3,1,2,0:T(8,128)S(1)}, f32[3,22,3,256]{3,1,2,0:T(8,128)S(1)}, u32[]{:S(2)}, u32[]{:S(2)}) collective-permute-start(f32[3,22,3,256]{3,1,2,0:T(8,128)S(1)} %get-tuple-element.595), channel_id=1, source_target_pairs={{8,0},{16,8},{24,16},{9,1},{17,9},{25,17},{10,2},{18,10},{26,18},{... | collective-permute-start | bytes 608264 | tf_op jit(solution)/shard_map/ppermute | solution.py:26
  45.1 10.4 %collective-permute-start.5 = (f32[3,22,22,3]{2,1,3,0:T(8,128)S(1)}, f32[3,22,22,3]{2,1,3,0:T(8,128)S(1)}, u32[]{:S(2)}, u32[]{:S(2)}) collective-permute-start(f32[3,22,22,3]{2,1,3,0:T(8,128)S(1)} %copy.135), channel_id=1, source_target_pairs={{1,0},{2,1},{3,2},{4,3},{5,4},{6,5},{7,6},{9,8},{10,9},{11,10},{12... | collective-permute-start | bytes 52280 | tf_op jit(solution)/shard_map/ppermute | solution.py:26
  117.3 15.3 %collective-permute-start.11 = (f32[3,16,16,3]{3,2,1,0:T(8,128)S(1)}, f32[3,16,16,3]{3,2,1,0:T(8,128)S(1)}, u32[]{:S(2)}, u32[]{:S(2)}) collective-permute-start(f32[3,16,16,3]{3,2,1,0:T(8,128)S(1)} %get-tuple-element.625), channel_id=1, source_target_pairs={{1,0},{2,1},{3,2},{4,3},{5,4},{6,5},{7,6},{9,8},{10,9},{11,10},{12... | collective-permute-start | bytes 27656 | tf_op jit(solution)/shard_map/ppermute | solution.py:49
  119.5 19.4 %collective-permute-start.10 = (f32[3,16,3,256]{3,2,1,0:T(4,128)S(1)}, f32[3,16,3,256]{3,2,1,0:T(4,128)S(1)}, u32[]{:S(2)}, u32[]{:S(2)}) collective-permute-start(f32[3,16,3,256]{3,2,1,0:T(4,128)S(1)} %get-tuple-element.627), channel_id=1, source_target_pairs={{8,0},{16,8},{24,16},{9,1},{17,9},{25,17},{10,2},{18,10},{26,18},{... | collective-permute-start | bytes 442376 | tf_op jit(solution)/shard_map/ppermute | solution.py:49
  120.8 18.1 %collective-permute-start.7 = (f32[3,16,3,256]{3,2,1,0:T(4,128)S(1)}, f32[3,16,3,256]{3,2,1,0:T(4,128)S(1)}, u32[]{:S(2)}, u32[]{:S(2)}) collective-permute-start(f32[3,16,3,256]{3,2,1,0:T(4,128)S(1)} %get-tuple-element.626), channel_id=1, source_target_pairs={{0,8},{8,16},{16,24},{1,9},{9,17},{17,25},{2,10},{10,18},{18,26},{... | collective-permute-start | bytes 442376 | tf_op jit(solution)/shard_map/ppermute | solution.py:48
  124.8 14.1 %collective-permute-start.6 = (f32[3,16,16,3]{3,2,1,0:T(8,128)S(1)}, f32[3,16,16,3]{3,2,1,0:T(8,128)S(1)}, u32[]{:S(2)}, u32[]{:S(2)}) collective-permute-start(f32[3,16,16,3]{3,2,1,0:T(8,128)S(1)} %get-tuple-element.624), channel_id=1, source_target_pairs={{0,1},{1,2},{2,3},{3,4},{4,5},{5,6},{6,7},{8,9},{9,10},{10,11},{11... | collective-permute-start | bytes 27656 | tf_op jit(solution)/shard_map/ppermute | solution.py:48
  128.7 10.3 %collective-permute-start.9 = (f32[3,3,16,256]{3,2,1,0:T(8,128)S(1)}, f32[3,3,16,256]{3,2,1,0:T(8,128)S(1)}, u32[]{:S(2)}, u32[]{:S(2)}) collective-permute-start(f32[3,3,16,256]{3,2,1,0:T(8,128)S(1)} %get-tuple-element.623), channel_id=1, source_target_pairs={{32,0},{64,32},{96,64},{33,1},{65,33},{97,65},{34,2},{66,34},{98,6... | collective-permute-start | bytes 442376 | tf_op jit(solution)/shard_map/ppermute | solution.py:49
  203.4 16.2 %collective-permute-start.17 = (f32[3,16,16,3]{3,2,1,0:T(8,128)S(1)}, f32[3,16,16,3]{3,2,1,0:T(8,128)S(1)}, u32[]{:S(2)}, u32[]{:S(2)}) collective-permute-start(f32[3,16,16,3]{3,2,1,0:T(8,128)S(1)} %get-tuple-element.617), channel_id=1, source_target_pairs={{1,0},{2,1},{3,2},{4,3},{5,4},{6,5},{7,6},{9,8},{10,9},{11,10},{12... | collective-permute-start | bytes 27656 | tf_op jit(solution)/shard_map/ppermute | solution.py:49
  205.7 20.7 %collective-permute-start.16 = (f32[3,16,3,256]{3,2,1,0:T(4,128)S(1)}, f32[3,16,3,256]{3,2,1,0:T(4,128)S(1)}, u32[]{:S(2)}, u32[]{:S(2)}) collective-permute-start(f32[3,16,3,256]{3,2,1,0:T(4,128)S(1)} %get-tuple-element.619), channel_id=1, source_target_pairs={{8,0},{16,8},{24,16},{9,1},{17,9},{25,17},{10,2},{18,10},{26,18},{... | collective-permute-start | bytes 442376 | tf_op jit(solution)/shard_map/ppermute | solution.py:49
  207.0 19.4 %collective-permute-start.13 = (f32[3,16,3,256]{3,2,1,0:T(4,128)S(1)}, f32[3,16,3,256]{3,2,1,0:T(4,128)S(1)}, u32[]{:S(2)}, u32[]{:S(2)}) collective-permute-start(f32[3,16,3,256]{3,2,1,0:T(4,128)S(1)} %get-tuple-element.618), channel_id=1, source_target_pairs={{0,8},{8,16},{16,24},{1,9},{9,17},{17,25},{2,10},{10,18},{18,26},{... | collective-permute-start | bytes 442376 | tf_op jit(solution)/shard_map/ppermute | solution.py:48
  211.3 15.1 %collective-permute-start.12 = (f32[3,16,16,3]{3,2,1,0:T(8,128)S(1)}, f32[3,16,16,3]{3,2,1,0:T(8,128)S(1)}, u32[]{:S(2)}, u32[]{:S(2)}) collective-permute-start(f32[3,16,16,3]{3,2,1,0:T(8,128)S(1)} %get-tuple-element.616), channel_id=1, source_target_pairs={{0,1},{1,2},{2,3},{3,4},{4,5},{5,6},{6,7},{8,9},{9,10},{10,11},{11... | collective-permute-start | bytes 27656 | tf_op jit(solution)/shard_map/ppermute | solution.py:48
  214.9 11.5 %collective-permute-start.15 = (f32[3,3,16,256]{3,2,1,0:T(8,128)S(1)}, f32[3,3,16,256]{3,2,1,0:T(8,128)S(1)}, u32[]{:S(2)}, u32[]{:S(2)}) collective-permute-start(f32[3,3,16,256]{3,2,1,0:T(8,128)S(1)} %get-tuple-element.615), channel_id=1, source_target_pairs={{32,0},{64,32},{96,64},{33,1},{65,33},{97,65},{34,2},{66,34},{98,6... | collective-permute-start | bytes 442376 | tf_op jit(solution)/shard_map/ppermute | solution.py:49
  294.2 16.0 %collective-permute-start.23 = (f32[3,16,16,3]{3,2,1,0:T(8,128)S(1)}, f32[3,16,16,3]{3,2,1,0:T(8,128)S(1)}, u32[]{:S(2)}, u32[]{:S(2)}) collective-permute-start(f32[3,16,16,3]{3,2,1,0:T(8,128)S(1)} %get-tuple-element.609), channel_id=1, source_target_pairs={{1,0},{2,1},{3,2},{4,3},{5,4},{6,5},{7,6},{9,8},{10,9},{11,10},{12... | collective-permute-start | bytes 27656 | tf_op jit(solution)/shard_map/ppermute | solution.py:49
  296.5 19.9 %collective-permute-start.22 = (f32[3,16,3,256]{3,2,1,0:T(4,128)S(1)}, f32[3,16,3,256]{3,2,1,0:T(4,128)S(1)}, u32[]{:S(2)}, u32[]{:S(2)}) collective-permute-start(f32[3,16,3,256]{3,2,1,0:T(4,128)S(1)} %get-tuple-element.611), channel_id=1, source_target_pairs={{8,0},{16,8},{24,16},{9,1},{17,9},{25,17},{10,2},{18,10},{26,18},{... | collective-permute-start | bytes 442376 | tf_op jit(solution)/shard_map/ppermute | solution.py:49
  297.8 18.6 %collective-permute-start.19 = (f32[3,16,3,256]{3,2,1,0:T(4,128)S(1)}, f32[3,16,3,256]{3,2,1,0:T(4,128)S(1)}, u32[]{:S(2)}, u32[]{:S(2)}) collective-permute-start(f32[3,16,3,256]{3,2,1,0:T(4,128)S(1)} %get-tuple-element.610), channel_id=1, source_target_pairs={{0,8},{8,16},{16,24},{1,9},{9,17},{17,25},{2,10},{10,18},{18,26},{... | collective-permute-start | bytes 442376 | tf_op jit(solution)/shard_map/ppermute | solution.py:48
  301.8 14.5 %collective-permute-start.18 = (f32[3,16,16,3]{3,2,1,0:T(8,128)S(1)}, f32[3,16,16,3]{3,2,1,0:T(8,128)S(1)}, u32[]{:S(2)}, u32[]{:S(2)}) collective-permute-start(f32[3,16,16,3]{3,2,1,0:T(8,128)S(1)} %get-tuple-element.608), channel_id=1, source_target_pairs={{0,1},{1,2},{2,3},{3,4},{4,5},{5,6},{6,7},{8,9},{9,10},{10,11},{11... | collective-permute-start | bytes 27656 | tf_op jit(solution)/shard_map/ppermute | solution.py:48
  305.6 10.7 %collective-permute-start.21 = (f32[3,3,16,256]{3,2,1,0:T(8,128)S(1)}, f32[3,3,16,256]{3,2,1,0:T(8,128)S(1)}, u32[]{:S(2)}, u32[]{:S(2)}) collective-permute-start(f32[3,3,16,256]{3,2,1,0:T(8,128)S(1)} %get-tuple-element.607), channel_id=1, source_target_pairs={{32,0},{64,32},{96,64},{33,1},{65,33},{97,65},{34,2},{66,34},{98,6... | collective-permute-start | bytes 442376 | tf_op jit(solution)/shard_map/ppermute | solution.py:49
  381.9 16.0 %collective-permute-start.29 = (f32[3,16,16,3]{3,2,1,0:T(8,128)S(1)}, f32[3,16,16,3]{3,2,1,0:T(8,128)S(1)}, u32[]{:S(2)}, u32[]{:S(2)}) collective-permute-start(f32[3,16,16,3]{3,2,1,0:T(8,128)S(1)} %get-tuple-element.601), channel_id=1, source_target_pairs={{1,0},{2,1},{3,2},{4,3},{5,4},{6,5},{7,6},{9,8},{10,9},{11,10},{12... | collective-permute-start | bytes 27656 | tf_op jit(solution)/shard_map/ppermute | solution.py:49
  384.2 20.5 %collective-permute-start.28 = (f32[3,16,3,256]{3,2,1,0:T(4,128)S(1)}, f32[3,16,3,256]{3,2,1,0:T(4,128)S(1)}, u32[]{:S(2)}, u32[]{:S(2)}) collective-permute-start(f32[3,16,3,256]{3,2,1,0:T(4,128)S(1)} %get-tuple-element.603), channel_id=1, source_target_pairs={{8,0},{16,8},{24,16},{9,1},{17,9},{25,17},{10,2},{18,10},{26,18},{... | collective-permute-start | bytes 442376 | tf_op jit(solution)/shard_map/ppermute | solution.py:49
  385.5 19.2 %collective-permute-start.25 = (f32[3,16,3,256]{3,2,1,0:T(4,128)S(1)}, f32[3,16,3,256]{3,2,1,0:T(4,128)S(1)}, u32[]{:S(2)}, u32[]{:S(2)}) collective-permute-start(f32[3,16,3,256]{3,2,1,0:T(4,128)S(1)} %get-tuple-element.602), channel_id=1, source_target_pairs={{0,8},{8,16},{16,24},{1,9},{9,17},{17,25},{2,10},{10,18},{18,26},{... | collective-permute-start | bytes 442376 | tf_op jit(solution)/shard_map/ppermute | solution.py:48
  389.5 15.2 %collective-permute-start.24 = (f32[3,16,16,3]{3,2,1,0:T(8,128)S(1)}, f32[3,16,16,3]{3,2,1,0:T(8,128)S(1)}, u32[]{:S(2)}, u32[]{:S(2)}) collective-permute-start(f32[3,16,16,3]{3,2,1,0:T(8,128)S(1)} %get-tuple-element.600), channel_id=1, source_target_pairs={{0,1},{1,2},{2,3},{3,4},{4,5},{5,6},{6,7},{8,9},{9,10},{10,11},{11... | collective-permute-start | bytes 27656 | tf_op jit(solution)/shard_map/ppermute | solution.py:48
  393.4 11.3 %collective-permute-start.27 = (f32[3,3,16,256]{3,2,1,0:T(8,128)S(1)}, f32[3,3,16,256]{3,2,1,0:T(8,128)S(1)}, u32[]{:S(2)}, u32[]{:S(2)}) collective-permute-start(f32[3,3,16,256]{3,2,1,0:T(8,128)S(1)} %get-tuple-element.599), channel_id=1, source_target_pairs={{32,0},{64,32},{96,64},{33,1},{65,33},{97,65},{34,2},{66,34},{98,6... | collective-permute-start | bytes 442376 | tf_op jit(solution)/shard_map/ppermute | solution.py:49
  (74 other events, 1256.9 us)
